TPU v7x, 32 devices: a whole 2x2x4 slice. The times are simulated.
32 devices in a mesh: dp: 8 (over z, y), mp: 4 (over x, core).
Axes of the slice: x: 2, y: 2, z: 4, core: 2. Of those that a mesh axis runs over, the one named last changes fastest.
Arguments:
- tokens: bfloat16 [8, 1024, 1280], P('dp', 'mp'), may hold values from -6 to 6
- sizes: float32 [8, 1024], P('dp'), may hold values from 1 to 8
- ln1_gain: float32 [1280], replicated, may hold values from 0.25 to 1.75
- qkv_weight: bfloat16 [3, 1280, 1280], P(None, 'dp', 'mp'), may hold values from -0.15625 to 0.15625
- proj_weight: bfloat16 [1280, 1280], P('mp', 'dp'), may hold values from -0.15625 to 0.15625
- ln2_gain: float32 [1280], replicated, may hold values from 0.25 to 1.75
- fc1_weight: bfloat16 [1280, 5120], P('dp', 'mp'), may hold values from -0.15625 to 0.15625
- fc1_bias: float32 [5120], P('mp'), may hold values from -3 to 3
- fc2_weight: bfloat16 [5120, 1280], P('mp', 'dp'), may hold values from -0.078125 to 0.078125
- pair_source: int32 [8, 16], P('dp'), may hold values from 0 to 1022, as said below
- pair_target: int32 [8, 16], P('dp'), may hold values from 1 to 1023, as said below
- kept_order: int32 [8, 1008], P('dp'), may hold values from 0 to 1023, as said below
Outputs:
- merged_out: bfloat16 [8, 1008, 1280], P('dp', 'mp')
Inputs may be any that keep to these rules, and one draw needn't show every extreme that they name: `pair_source`: in each image the 16 entries are distinct even token indices. `pair_target`: odd token indices; several sources may join the same target. `kept_order`: in each image every token index that is not in pair_source appears exactly once.
All inputs are finite; a program needn't handle non-finite values.
Results may differ from a plain program's by a relative error of at most 0.017.
Values may be sent and summed in bfloat16 or wider, within the bound.
A program may use at most 64 MiB of HBM per device.

v0:
```python
import math
import jax
import jax.numpy as jnp
from jax import lax
from jax.sharding import PartitionSpec as P

D = 1280
HEADS = 16


def layer_norm(values, gain):
    center = values - jnp.mean(values, axis=-1, keepdims=True)
    spread = jnp.mean(center * center, axis=-1, keepdims=True)
    return center * lax.rsqrt(spread + 1e-06) * gain


def merge_rows(total, order_rows, source_ids, target_ids):
    kept_rows = jnp.take_along_axis(total, order_rows[:, :, None], axis=1)
    source_rows = jnp.take_along_axis(total, source_ids[:, :, None], axis=1)
    joins = (order_rows[:, :, None] == target_ids[:, None, :]).astype(jnp.float32)
    return kept_rows + jnp.einsum(
        "icr,ird->icd", joins, source_rows, precision=lax.Precision.HIGHEST
    )


def shards(
    tokens,
    sizes,
    ln1_gain,
    qkv_weight,
    proj_weight,
    ln2_gain,
    fc1_weight,
    fc1_bias,
    fc2_weight,
    pair_source,
    pair_target,
    kept_order,
):
    images, own_tokens, width = tokens.shape
    length = sizes.shape[1]
    kept_total = kept_order.shape[1]
    devices_mp = lax.axis_size("mp")
    own_start = lax.axis_index("mp") * own_tokens
    head_size = D // HEADS
    base = tokens.astype(jnp.float32)
    normed = layer_norm(base, ln1_gain).astype(jnp.bfloat16)
    whole = lax.all_gather(normed, "mp", axis=1, tiled=True)
    local_width = qkv_weight.shape[2]
    columns = whole
    projected = jnp.einsum(
        "ind,cdf->cinf",
        columns,
        lax.all_gather(qkv_weight, "dp", axis=1, tiled=True),
        preferred_element_type=jnp.float32,
    ).astype(jnp.bfloat16)
    local_heads = local_width // head_size
    shaped = projected.reshape(3, images, length, local_heads, head_size)
    queries = shaped[0]
    keys_all = shaped[1]
    values_all = shaped[2]
    size_bias = jnp.log(sizes)[:, None, None, :]
    block = min(512, length)
    outputs = []
    for begin in range(0, length, block):
        scores = (
            jnp.einsum(
                "iqhe,ikhe->ihqk",
                queries[:, begin : begin + block],
                keys_all,
                preferred_element_type=jnp.float32,
            )
            / math.sqrt(head_size)
            + size_bias
        )
        weights = jax.nn.softmax(scores, axis=-1).astype(jnp.bfloat16)
        attended_block = jnp.einsum(
            "ihqk,ikhe->iqhe", weights, values_all, preferred_element_type=jnp.float32
        )
        outputs.append(attended_block.astype(jnp.bfloat16).reshape(images, block, local_width))
    attended = jnp.concatenate(outputs, axis=1)
    branch = jnp.einsum(
        "ind,de->ine",
        attended,
        lax.all_gather(proj_weight, "dp", axis=1, tiled=True),
        preferred_element_type=jnp.float32,
    )
    weighted = sizes[:, :, None] * branch
    own_sizes = lax.dynamic_slice_in_dim(sizes, own_start, own_tokens, 1)
    own_weighted = own_sizes[:, :, None] * base
    local_total = lax.dynamic_update_slice_in_dim(
        weighted,
        lax.dynamic_slice_in_dim(weighted, own_start, own_tokens, 1) + own_weighted,
        own_start,
        1,
    )
    merged_count = kept_total // devices_mp
    own_order = lax.dynamic_slice_in_dim(
        kept_order, lax.axis_index("mp") * merged_count, merged_count, 1
    )
    scattered = lax.psum_scatter(
        jnp.transpose(
            merge_rows(local_total, kept_order, pair_source, pair_target), (1, 0, 2)
        ).astype(jnp.bfloat16),
        "mp",
        scatter_dimension=0,
        tiled=True,
    ).astype(jnp.float32)
    numerator = jnp.transpose(scattered, (1, 0, 2))
    merged_size = merge_rows(sizes[:, :, None], own_order, pair_source, pair_target)
    merged = numerator / merged_size
    normed_two = layer_norm(merged, ln2_gain).astype(jnp.bfloat16)
    gathered = lax.all_gather(normed_two, "mp", axis=1, tiled=True)
    columns = gathered
    hidden_sum = jnp.einsum(
        "imd,df->imf",
        columns,
        lax.all_gather(fc1_weight, "dp", axis=0, tiled=True),
        preferred_element_type=jnp.float32,
    )
    hidden = jax.nn.gelu(hidden_sum + fc1_bias).astype(jnp.bfloat16)
    partial_out = jnp.einsum(
        "imf,fd->imd",
        hidden,
        lax.all_gather(fc2_weight, "dp", axis=1, tiled=True),
        preferred_element_type=jnp.float32,
    )
    mlp_part = lax.psum_scatter(
        partial_out.astype(jnp.bfloat16), "mp", scatter_dimension=1, tiled=True
    ).astype(jnp.float32)
    return (merged + mlp_part).astype(jnp.bfloat16)


def solution(mesh):
    return jax.shard_map(
        shards,
        mesh=mesh,
        in_specs=(
            P("dp", "mp", None),
            P("dp", None),
            P(),
            P(None, "dp", "mp"),
            P("mp", "dp"),
            P(),
            P("dp", "mp"),
            P("mp"),
            P("mp", "dp"),
            P("dp", None),
            P("dp", None),
            P("dp", None),
        ),
        out_specs=P("dp", "mp", None),
        check_vma=False,
    )
```

profile of v0, /device:TPU:1, one launch (start us, length us, event | category | flops | bytes accessed | tf_op | source)
XLA Modules:
  0.0 317.7 jit_solution(4380768634615341311)
XLA Ops:
  6.5 0.0 all-gather.6.cloned.1.call-start
  6.6 1.3 convert_reduce_fusion
  7.9 0.0 copy-start.5
  7.9 1.4 fusion.30
  9.3 2.2 fusion.32
  11.5 0.0 all-gather.6.cloned.1.call-update
  11.6 0.0 all-gather.8.cloned.1.call-start
  11.6 0.7 all-gather.8.cloned.1.call-update
  12.3 0.0 all-gather.12.cloned.1.call-start
  12.4 0.7 all-gather.12.cloned.1.call-update
  13.0 0.0 all-gather.14.cloned.1.call-start
  13.1 0.5 all-gather.14.cloned.1.call-update
  13.6 0.0 all-gather.10.cloned.1.call-start
  13.7 0.0 copy-done.8
  13.7 0.0 copy-done
  13.7 0.0 copy-done.2
  13.8 28.3 %all_gather.20 = bf16[320,1280]{0,1:T(8,128)(2,1)S(1)} all-gather(bf16[320,160]{0,1:T(8,128)(2,1)S(1)} %copy-done.2), channel_id=1, replica_groups=mesh['dp'=8,'mp'=4] {'dp'}, dimensions={1}, use_global_device_ids=true | all-gather | bytes 921600 | tf_op jit(solution)/shard_map/all_gather | solution.py:85
  42.0 0.0 copy-done.3
  42.1 0.1 compare_select_fusion.2
  42.2 0.6 gather_fusion.3
  42.8 1.4 gather_fusion.2
  44.2 0.0 copy-done.5
  44.2 0.2 fusion.56
  44.4 53.4 %all-gather.8.cloned.1.call-done = bf16[3,1280,320]{2,1,0:T(8,128)(2,1)} async-done(((bf16[3,160,320]{2,1,0:T(8,128)(2,1)}), bf16[3,1280,320]{2,1,0:T(8,128)(2,1)}) %all-gather.8.cloned.1.call-update) | async-done | bytes 2457616 | tf_op jit(solution)/shard_map/all_gather | solution.py:54
  97.8 5.4 %convert_bitcast_fusion = bf16[3,1,1024,320]{2,3,0,1:T(8,128)(2,1)S(1)} fusion(bf16[3,1280,320]{2,1,0:T(8,128)(2,1)} %all-gather.8.cloned.1.call-done, bf16[1,1024,1280]{2,1,0:T(8,128)(2,1)} %all-gather.6.cloned.1.call-done), kind=kOutput, calls=%fused_computation.38 | convolution fusion | flops 2517565440 | bytes 7045120 | tf_op jit(solution)/shard_map/ind,cdf->cinf/dot_general | solution.py:51
  103.2 0.2 fusion.78
  103.3 4.9 %fusion.80 = (f32[4,512]{1,0:T(4,128)S(1)}, f32[4,512,1024]{2,1,0:T(8,128)}) fusion(f32[1024]{0:T(1024)S(1)} %bitcast.179, bf16[1024,4,80]{0,2,1:T(8,128)(2,1)S(1)} %bitcast.170, bf16[1,1024,4,80]{1,3,2,0:T(8,128)(2,1)S(1)} %bitcast.168), kind=kOutput, calls=%fused_computation.120 | convolution fusion | flops 343933952 | bytes 9383936 | tf_op jit(solution)/shard_map/sub | solution.py:76
  108.2 4.9 %fusion.79 = (f32[4,512]{1,0:T(4,128)S(1)}, f32[4,512,1024]{2,1,0:T(8,128)}) fusion(f32[1024]{0:T(1024)S(1)} %bitcast.180, bf16[1024,4,80]{0,2,1:T(8,128)(2,1)S(1)} %bitcast.171, bf16[1,1024,4,80]{1,3,2,0:T(8,128)(2,1)S(1)} %bitcast.169), kind=kOutput, calls=%fused_computation.119 | convolution fusion | flops 343933952 | bytes 9383936 | tf_op jit(solution)/shard_map/sub | solution.py:76
  113.0 5.1 %fusion.37 = bf16[4,80,512]{2,1,0:T(8,128)(2,1)S(1)} fusion(bf16[1024,4,80]{0,2,1:T(8,128)(2,1)S(1)} %bitcast.166, f32[4,512,1024]{2,1,0:T(8,128)} %get-tuple-element.13, f32[4,512]{1,0:T(4,128)S(1)} %get-tuple-element.12), kind=kOutput, calls=%fused_computation.55 | convolution fusion | flops 339902464 | bytes 9379840 | tf_op jit(solution)/shard_map/ihqk,ikhe->iqhe/dot_general | solution.py:77
  118.1 0.8 copy-done.9
  118.9 1.7 fusion.36
  120.6 0.0 copy-start.1
  120.6 4.0 %convolution_multiply_fusion = f32[1024,1280]{1,0:T(8,128)} fusion(bf16[320,1280]{0,1:T(8,128)(2,1)S(1)} %all_gather.20, f32[1024]{0:T(1024)S(1)} %bitcast.165, bf16[1,512,320]{1,2,0:T(8,128)(2,1)S(1)} %bitcast.173, bf16[1,512,320]{1,2,0:T(8,128)(2,1)S(1)} %bitcast.172), kind=kOutput, calls=%fused_computation.24 | convolution fusion | flops 841482240 | bytes 6721536 | tf_op jit(solution)/shard_map/ind,de->ine/dot_general | solution.py:82
  124.6 1.4 constant_dynamic-slice_fusion.2
  126.0 0.0 copy-done.1
  126.0 1.3 fusion.35
  127.3 3.1 gather_fusion.1
  130.5 9.7 %gather_fusion = f32[1008,1280]{1,0:T(8,128)} fusion(f32[1024,1280]{1,0:T(8,128)} %fusion.35, s32[1024]{0:T(1024)S(1)} %pad_clamp_fusion.2), kind=kCustom, calls=%fused_computation | custom fusion | bytes 10325952 | tf_op jit(solution)/shard_map/jit(take_along_axis)/gather | solution.py:18
  140.1 5.1 %fusion.21 = bf16[1008,1,1280]{2,0,1:T(8,128)(2,1)S(1)} fusion(f32[1008,1280]{1,0:T(8,128)} %gather_fusion, pred[1008]{0:T(1024)(128)(4,1)S(1)} %compare_and_fusion, f32[16,1280]{1,0:T(8,128)S(1)} %gather_fusion.1, pred[16]{0:T(512)(128)(4,1)S(1)} %compare_and_fusion.1, s32[1008]{0:T(1024)S(1)} %bitcast.175, s32[16]{0:T(128)S(1)} %bitcast.185), kind=kOutput, calls=%fused_computation.33 | convolution fusion | flops 251633408 | bytes 7828480 | tf_op jit(solution)/shard_map/icr,ird->icd/dot_general | solution.py:21
  145.2 0.0 copy-start.6
  145.2 0.0 copy-start.4
  145.2 27.6 %fusion = bf16[256,1280]{1,0:T(8,128)(2,1)S(1)} fusion(bf16[1008,1,1280]{2,0,1:T(8,128)(2,1)S(1)} %fusion.21), kind=kCustom, calls=%all-reduce-scatter | all-reduce-scatter fusion | flops 1310721 | bytes 3236352
  172.8 4.4 %collective-permute-start = (bf16[12,1280]{1,0:T(8,128)(2,1)S(1)}, bf16[12,1280]{1,0:T(8,128)(2,1)S(1)}, u32[]{:S(2)}, u32[]{:S(2)}) collective-permute-start(bf16[12,1280]{1,0:T(8,128)(2,1)S(1)} %slice.36), channel_id=1, source_target_pairs={{0,1},{1,2},{2,3},{4,5},{5,6},{6,7},{8,9},{9,10},{10,11},{12,13},{... | collective-permute-start | bytes 92168
  177.2 0.0 copy-done.6
  177.2 0.6 dynamic-slice.10
  178.5 0.0 collective-permute-done
  178.5 1.1 concatenate.4
  179.6 0.0 copy-start.7
  179.6 0.4 fusion.46
  180.0 0.5 multiply_reduce_fusion
  180.5 0.0 copy-done.4
  180.5 0.4 multiply_convert_fusion
  180.9 2.1 copy.14
  183.0 0.0 all-gather.10.cloned.1.call-update
  183.0 0.0 all-gather.12.cloned.1.call-done
  183.1 39.2 %all-gather.14.cloned.1.call-done = bf16[1280,1280]{0,1:T(8,128)(2,1)} async-done(((bf16[1280,160]{0,1:T(8,128)(2,1)}), bf16[1280,1280]{0,1:T(8,128)(2,1)}) %all-gather.14.cloned.1.call-update) | async-done | bytes 3276816 | tf_op jit(solution)/shard_map/all_gather | solution.py:125
  222.2 42.2 %all-gather.10.cloned.1.call-done = bf16[1,1008,1280]{2,0,1:T(2,128)(2,1)} async-done(((bf16[1,252,1280]{2,0,1:T(2,128)(2,1)}), bf16[1,1008,1280]{2,0,1:T(2,128)(2,1)}) %all-gather.10.cloned.1.call-update) | async-done | bytes 2580496 | tf_op jit(solution)/shard_map/all_gather | solution.py:113
  264.5 0.0 copy-done.7
  264.5 12.8 %fusion.20 = bf16[1,1008,1280]{2,1,0:T(8,128)(2,1)} fusion(bf16[1280,1280]{0,1:T(8,128)(2,1)} %all-gather.14.cloned.1.call-done, bf16[1280,1280]{1,0:T(8,128)(2,1)} %all-gather.12.cloned.1.call-done, bf16[1,1008,1280]{2,0,1:T(2,128)(2,1)} %all-gather.10.cloned.1.call-done, f32[1280]{0:T(1024)S(1)} %copy-done.7), kind=kOutput, calls=%fused_computation.32 | convolution fusion | flops 6620221440 | bytes 11719680 | tf_op jit(solution)/shard_map/imf,fd->imd/dot_general | solution.py:122
  277.3 26.0 %fusion.1 = bf16[256,1280]{1,0:T(8,128)(2,1)S(1)} fusion(bf16[1,1008,1280]{2,1,0:T(8,128)(2,1)} %fusion.20), kind=kCustom, calls=%all-reduce-scatter.1 | all-reduce-scatter fusion | flops 1310721 | bytes 3236352
  303.4 4.4 %collective-permute-start.1 = (bf16[12,1280]{1,0:T(8,128)(2,1)S(1)}, bf16[12,1280]{1,0:T(8,128)(2,1)S(1)}, u32[]{:S(2)}, u32[]{:S(2)}) collective-permute-start(bf16[12,1280]{1,0:T(8,128)(2,1)S(1)} %slice.37), channel_id=1, source_target_pairs={{0,1},{1,2},{2,3},{4,5},{5,6},{6,7},{8,9},{9,10},{10,11},{12,13},{... | collective-permute-start | bytes 92168
  307.8 1.1 collective-permute-done.1
  308.9 1.0 concatenate.5
  309.9 1.3 add_convert_fusion.1
  (22 shorter events, 0.1 us)
Async XLA Ops:
  6.5 7.1 %copy-start.8 = (s32[1,16]{1,0:T(1,128)S(1)}, s32[1,16]{1,0:T(1,128)}, u32[]{:S(2)}) copy-start(s32[1,16]{1,0:T(1,128)} %param.21) | copy-start | bytes 196
  6.5 7.2 %copy-start = (f32[1,1024]{1,0:T(1,128)S(1)}, f32[1,1024]{1,0:T(1,128)}, u32[]{:S(2)}) copy-start(f32[1,1024]{1,0:T(1,128)} %param.13) | copy-start | bytes 12292
  6.5 7.2 %copy-start.2 = (bf16[320,160]{0,1:T(8,128)(2,1)S(1)}, bf16[320,160]{0,1:T(8,128)(2,1)}, u32[]{:S(2)}) copy-start(bf16[320,160]{0,1:T(8,128)(2,1)} %param.16) | copy-start | bytes 307204
  6.5 35.5 %copy-start.3 = (s32[1,1008]{1,0:T(1,128)S(1)}, s32[1,1008]{1,0:T(1,128)}, u32[]{:S(2)}) copy-start(s32[1,1008]{1,0:T(1,128)} %param.23) | copy-start | bytes 12100
  6.5 37.8 %all-gather.6.cloned.1.call-start = ((), (), s32[]{:S(2)}) async-start(), calls=%async_computation | async-start | bytes 3276800 | tf_op jit(solution)/shard_map/all_gather | solution.py:48
  7.9 36.3 %copy-start.5 = (s32[1,16]{1,0:T(1,128)S(1)}, s32[1,16]{1,0:T(1,128)}, u32[]{:S(2)}) copy-start(s32[1,16]{1,0:T(1,128)} %param.22) | copy-start | bytes 196
  11.6 86.2 %all-gather.8.cloned.1.call-start = ((), (), s32[]{:S(2)}) async-start(), calls=%async_computation.1 | async-start | bytes 3317760 | tf_op jit(solution)/shard_map/all_gather | solution.py:54
  12.3 170.7 %all-gather.12.cloned.1.call-start = ((), (), s32[]{:S(2)}) async-start(), calls=%async_computation.3 | async-start | bytes 3686400 | tf_op jit(solution)/shard_map/all_gather | solution.py:118
  13.0 209.2 %all-gather.14.cloned.1.call-start = ((), (), s32[]{:S(2)}) async-start(), calls=%async_computation.4 | async-start | bytes 3686400 | tf_op jit(solution)/shard_map/all_gather | solution.py:125
  13.6 250.8 %all-gather.10.cloned.1.call-start = ((), (), s32[]{:S(2)}) async-start(), calls=%async_computation.2 | async-start | bytes 6451200 | tf_op jit(solution)/shard_map/all_gather | solution.py:113
  113.0 5.9 %copy-start.9 = (f32[4,512,1024]{2,1,0:T(8,128)S(1)}, f32[4,512,1024]{2,1,0:T(8,128)}, u32[]{:S(2)}) copy-start(f32[4,512,1024]{2,1,0:T(8,128)} %get-tuple-element.11) | copy-start | bytes 25165828
  120.6 5.4 %copy-start.1 = (bf16[1,256,1280]{2,1,0:T(8,128)(2,1)S(1)}, bf16[1,256,1280]{2,1,0:T(8,128)(2,1)}, u32[]{:S(2)}) copy-start(bf16[1,256,1280]{2,1,0:T(8,128)(2,1)} %param.12) | copy-start | bytes 1966084
  145.2 32.0 %copy-start.6 = (u32[32]{0:T(128)S(1)}, u32[32]{0:T(128)}, u32[]{:S(2)}) copy-start(u32[32]{0:T(128)} %constant.99) | copy-start | bytes 388
  145.2 35.3 %copy-start.4 = (f32[1280]{0:T(1024)S(1)}, f32[1280]{0:T(1024)}, u32[]{:S(2)}) copy-start(f32[1280]{0:T(1024)} %param.17) | copy-start | bytes 15364
  172.8 5.7 %collective-permute-start = (bf16[12,1280]{1,0:T(8,128)(2,1)S(1)}, bf16[12,1280]{1,0:T(8,128)(2,1)S(1)}, u32[]{:S(2)}, u32[]{:S(2)}) collective-permute-start(bf16[12,1280]{1,0:T(8,128)(2,1)S(1)} %slice.36), channel_id=1, source_target_pairs={{0,1},{1,2},{2,3},{4,5},{5,6},{6,7},{8,9},{9,10},{10,11},{12,13},{... | collective-permute-start | bytes 92168
  179.6 84.9 %copy-start.7 = (f32[1280]{0:T(1024)S(1)}, f32[1280]{0:T(1024)}, u32[]{:S(2)}) copy-start(f32[1280]{0:T(1024)} %param.19) | copy-start | bytes 15364
  303.4 5.5 %collective-permute-start.1 = (bf16[12,1280]{1,0:T(8,128)(2,1)S(1)}, bf16[12,1280]{1,0:T(8,128)(2,1)S(1)}, u32[]{:S(2)}, u32[]{:S(2)}) collective-permute-start(bf16[12,1280]{1,0:T(8,128)(2,1)S(1)} %slice.37), channel_id=1, source_target_pairs={{0,1},{1,2},{2,3},{4,5},{5,6},{6,7},{8,9},{9,10},{10,11},{12,13},{... | collective-permute-start | bytes 92168
Sparse Core Ops, SparseCore 0:
  11.7 27.9 all-gather.5
  41.9 55.8 all-gather.7
  100.0 59.9 all-gather.11
  162.0 60.1 all-gather.13
  223.6 40.7 all-gather.9
where the time goes:
time: 318 us
  waiting for transfers between devices  138 us (43%)
  blocking collectives  81.9 us (26%)
  matrix products  44 us (14%)
  local copies, waits for them, and re-layouts  22 us (7%)
  between operations  14.1 us (4%)
  starting transfers between devices  8.96 us (3%)
  other arithmetic  8.93 us (3%)
    unnamed x2, blocking collectives  53.6 us
    all_gather x1, waiting for transfers between devices, shards(): lax.all_gather(qkv_weight, 'dp', axis=1, tiled=True)  53.4 us
    all_gather x1, waiting for transfers between devices, shards(): gathered = lax.all_gather(normed_two, 'mp', axis=1, tiled=True)  42.2 us
    all_gather x1, waiting for transfers between devices, shards(): lax.all_gather(fc2_weight, 'dp', axis=1, tiled=True)  39.2 us
    all_gather x1, blocking collectives, shards(): lax.all_gather(proj_weight, 'dp', axis=1, tiled=True)  28.3 us
    dot_general x1, matrix products, shards(): jnp.einsum('imf,fd->imd', hidden, lax.all_gather(fc2_weight, 'dp', axis=1...  12.8 us
    gather x2, local copies, waits for them, and re-layouts, merge_rows(): kept_rows = jnp.take_along_axis(total, order_rows[:, :, None], axis=1)  11 us
    sub x2, matrix products, shards(): weights = jax.nn.softmax(scores, axis=-1).astype(jnp.bfloat16)  9.7 us
  transfers between devices with their start and end apart: 7, of which 4 were waited for; matrix products, arithmetic and copies ran while one was open for 26% of the time, Pallas kernels for 0%

commit v1 on v0

--- a/solution.py
+++ b/solution.py
@@ -110,7 +110,8 @@
     merged_size = merge_rows(sizes[:, :, None], own_order, pair_source, pair_target)
     merged = numerator / merged_size
     normed_two = layer_norm(merged, ln2_gain).astype(jnp.bfloat16)
-    gathered = lax.all_gather(normed_two, "mp", axis=1, tiled=True)
+    carry = lax.all_gather(normed_two, "mp")
+    gathered = jnp.concatenate(carry, axis=1)
     columns = gathered
     hidden_sum = jnp.einsum(
         "imd,df->imf",

time: 318 us -> 384 us (1.21)
  waiting for transfers between devices: 138 us -> 203 us
    all_gather x1, waiting for transfers between devices: 0.02 us -> 59.4 us  [shards(): lax.all_gather(fc1_weight, 'dp', axis=0, tiled=True)]
    all_gather x1, waiting for transfers between devices: 39.2 us -> 62.2 us  [shards(): lax.all_gather(fc2_weight, 'dp', axis=1, tiled=True)]
    all_gather x1, waiting for transfers between devices: 42.2 us -> 23.9 us  [shards(): carry = lax.all_gather(normed_two, 'mp')]
  transfers between devices with their start and end apart: 7 -> 7, of which waited for: 4 -> 5; matrix products, arithmetic and copies ran while one was open for 26% -> 1% of each run, Pallas kernels for 0% -> 0%
where the time goes in v1:
time: 384 us
  waiting for transfers between devices  203 us (53%)
  blocking collectives  83.5 us (22%)
  matrix products  42.9 us (11%)
  local copies, waits for them, and re-layouts  21.7 us (6%)
  between operations  14.1 us (4%)
  other arithmetic  9.75 us (3%)
  starting transfers between devices  8.97 us (2%)
    all_gather x1, waiting for transfers between devices, shards(): lax.all_gather(fc2_weight, 'dp', axis=1, tiled=True)  62.2 us
    all_gather x1, waiting for transfers between devices, shards(): lax.all_gather(fc1_weight, 'dp', axis=0, tiled=True)  59.4 us
    unnamed x2, blocking collectives  55.1 us
    all_gather x1, waiting for transfers between devices, shards(): lax.all_gather(qkv_weight, 'dp', axis=1, tiled=True)  54.6 us
    all_gather x1, blocking collectives, shards(): lax.all_gather(proj_weight, 'dp', axis=1, tiled=True)  28.3 us
    all_gather x1, waiting for transfers between devices, shards(): carry = lax.all_gather(normed_two, 'mp')  23.9 us
    dot_general x1, matrix products, shards(): jnp.einsum('imf,fd->imd', hidden, lax.all_gather(fc2_weight, 'dp', axis=1...  11.7 us
    gather x2, local copies, waits for them, and re-layouts, merge_rows(): kept_rows = jnp.take_along_axis(total, order_rows[:, :, None], axis=1)  10.9 us
  transfers between devices with their start and end apart: 7, of which 5 were waited for; matrix products, arithmetic and copies ran while one was open for 1% of the time, Pallas kernels for 0%

profile of v1, /device:TPU:1, one launch (start us, length us, event | category | flops | bytes accessed | tf_op | source)
XLA Modules:
  0.0 383.9 jit_solution(10635563699653789839)
XLA Ops:
  6.5 0.0 copy-start
  6.5 0.0 copy-start.8
  6.5 0.0 all-gather.6.cloned.1.call-start
  6.6 1.3 convert_reduce_fusion
  7.9 1.4 fusion.28
  9.3 2.2 fusion.30
  11.5 0.0 all-gather.6.cloned.1.call-update
  11.6 0.0 all-gather.8.cloned.1.call-start
  11.6 0.7 all-gather.8.cloned.1.call-update
  12.3 0.0 all-gather.10.cloned.1.call-start
  12.4 0.0 copy-done
  12.4 0.0 copy-done.8
  12.4 0.6 gather_fusion.3
  13.1 0.0 copy-done.3
  13.1 0.1 compare_select_fusion.2
  13.2 1.4 gather_fusion.2
  14.6 0.0 copy-done.5
  14.6 0.2 fusion.58
  14.8 0.0 copy-done.2
  14.8 28.3 %all_gather.21 = bf16[320,1280]{0,1:T(8,128)(2,1)S(1)} all-gather(bf16[320,160]{0,1:T(8,128)(2,1)S(1)} %copy-done.2), channel_id=1, replica_groups=mesh['dp'=8,'mp'=4] {'dp'}, dimensions={1}, use_global_device_ids=true | all-gather | bytes 921600 | tf_op jit(solution)/shard_map/all_gather | solution.py:85
  43.2 54.6 %all-gather.8.cloned.1.call-done = bf16[3,1280,320]{2,1,0:T(8,128)(2,1)} async-done(((bf16[3,160,320]{2,1,0:T(8,128)(2,1)}), bf16[3,1280,320]{2,1,0:T(8,128)(2,1)}) %all-gather.8.cloned.1.call-update) | async-done | bytes 2457616 | tf_op jit(solution)/shard_map/all_gather | solution.py:54
  97.8 5.4 %convert_bitcast_fusion = bf16[3,1,1024,320]{2,3,0,1:T(8,128)(2,1)S(1)} fusion(bf16[3,1280,320]{2,1,0:T(8,128)(2,1)} %all-gather.8.cloned.1.call-done, bf16[1,1024,1280]{2,1,0:T(8,128)(2,1)} %all-gather.6.cloned.1.call-done), kind=kOutput, calls=%fused_computation.36 | convolution fusion | flops 2517565440 | bytes 7045120 | tf_op jit(solution)/shard_map/ind,cdf->cinf/dot_general | solution.py:51
  103.2 0.2 fusion.80
  103.3 5.0 %fusion.82 = (f32[4,512]{1,0:T(4,128)S(1)}, f32[4,512,1024]{2,1,0:T(8,128)}) fusion(f32[1024]{0:T(1024)S(1)} %bitcast.181, bf16[1024,4,80]{0,2,1:T(8,128)(2,1)S(1)} %bitcast.172, bf16[1,1024,4,80]{1,3,2,0:T(8,128)(2,1)S(1)} %bitcast.170), kind=kOutput, calls=%fused_computation.123 | convolution fusion | flops 343933952 | bytes 9383936 | tf_op jit(solution)/shard_map/sub | solution.py:76
  108.4 4.9 %fusion.81 = (f32[4,512]{1,0:T(4,128)S(1)}, f32[4,512,1024]{2,1,0:T(8,128)}) fusion(f32[1024]{0:T(1024)S(1)} %bitcast.182, bf16[1024,4,80]{0,2,1:T(8,128)(2,1)S(1)} %bitcast.173, bf16[1,1024,4,80]{1,3,2,0:T(8,128)(2,1)S(1)} %bitcast.171), kind=kOutput, calls=%fused_computation.122 | convolution fusion | flops 343933952 | bytes 9383936 | tf_op jit(solution)/shard_map/sub | solution.py:76
  113.2 5.0 %fusion.41 = bf16[4,80,512]{2,1,0:T(8,128)(2,1)S(1)} fusion(bf16[1024,4,80]{0,2,1:T(8,128)(2,1)S(1)} %bitcast.168, f32[4,512,1024]{2,1,0:T(8,128)} %get-tuple-element.13, f32[4,512]{1,0:T(4,128)S(1)} %get-tuple-element.12), kind=kOutput, calls=%fused_computation.59 | convolution fusion | flops 339902464 | bytes 9379840 | tf_op jit(solution)/shard_map/ihqk,ikhe->iqhe/dot_general | solution.py:77
  118.2 0.7 copy-done.9
  119.0 1.7 fusion.40
  120.7 0.0 copy-start.1
  120.7 4.0 %convolution_multiply_fusion = f32[1024,1280]{1,0:T(8,128)} fusion(bf16[320,1280]{0,1:T(8,128)(2,1)S(1)} %all_gather.21, f32[1024]{0:T(1024)S(1)} %bitcast.167, bf16[1,512,320]{1,2,0:T(8,128)(2,1)S(1)} %bitcast.175, bf16[1,512,320]{1,2,0:T(8,128)(2,1)S(1)} %bitcast.174), kind=kOutput, calls=%fused_computation.24 | convolution fusion | flops 841482240 | bytes 6721536 | tf_op jit(solution)/shard_map/ind,de->ine/dot_general | solution.py:82
  124.7 1.4 constant_dynamic-slice_fusion.2
  126.1 0.0 copy-done.1
  126.1 1.3 fusion.39
  127.4 3.1 gather_fusion.1
  130.6 9.5 %gather_fusion = f32[1008,1280]{1,0:T(8,128)} fusion(f32[1024,1280]{1,0:T(8,128)} %fusion.39, s32[1024]{0:T(1024)S(1)} %pad_clamp_fusion.2), kind=kCustom, calls=%fused_computation | custom fusion | bytes 10325952 | tf_op jit(solution)/shard_map/jit(take_along_axis)/gather | solution.py:18
  140.1 5.1 %fusion.21 = bf16[1008,1,1280]{2,0,1:T(8,128)(2,1)S(1)} fusion(f32[1008,1280]{1,0:T(8,128)} %gather_fusion, pred[1008]{0:T(1024)(128)(4,1)S(1)} %compare_and_fusion, f32[16,1280]{1,0:T(8,128)S(1)} %gather_fusion.1, pred[16]{0:T(512)(128)(4,1)S(1)} %compare_and_fusion.1, s32[1008]{0:T(1024)S(1)} %bitcast.177, s32[16]{0:T(128)S(1)} %bitcast.187), kind=kOutput, calls=%fused_computation.33 | convolution fusion | flops 251633408 | bytes 7828480 | tf_op jit(solution)/shard_map/icr,ird->icd/dot_general | solution.py:21
  145.1 0.0 copy-start.6
  145.1 0.0 copy-start.4
  145.2 27.3 %fusion = bf16[256,1280]{1,0:T(8,128)(2,1)S(1)} fusion(bf16[1008,1,1280]{2,0,1:T(8,128)(2,1)S(1)} %fusion.21), kind=kCustom, calls=%all-reduce-scatter | all-reduce-scatter fusion | flops 1310721 | bytes 3236352
  172.5 4.4 %collective-permute-start = (bf16[12,1280]{1,0:T(8,128)(2,1)S(1)}, bf16[12,1280]{1,0:T(8,128)(2,1)S(1)}, u32[]{:S(2)}, u32[]{:S(2)}) collective-permute-start(bf16[12,1280]{1,0:T(8,128)(2,1)S(1)} %slice.36), channel_id=1, source_target_pairs={{0,1},{1,2},{2,3},{4,5},{5,6},{6,7},{8,9},{9,10},{10,11},{12,13},{... | collective-permute-start | bytes 92168
  176.9 0.0 copy-done.6
  176.9 0.6 dynamic-slice.10
  178.1 0.0 collective-permute-done
  178.2 1.1 concatenate.4
  179.2 0.4 fusion.48
  179.7 0.5 multiply_reduce_fusion
  180.1 0.0 copy-done.4
  180.1 1.2 fusion.36
  181.4 0.0 all-gather.10.cloned.1.call-update
  181.4 0.0 all-gather.12.cloned.1.call-start
  181.5 0.5 all-gather.12.cloned.1.call-update
  182.0 0.0 all-gather.14.cloned.1.call-start
  182.0 0.5 all-gather.14.cloned.1.call-update
  182.6 23.9 %all-gather.10.cloned.1.call-done = bf16[4,1,252,1280]{3,2,1,0:T(8,128)(2,1)} async-done(((bf16[1,1,252,1280]{3,2,1,0:T(8,128)(2,1)}), bf16[4,1,252,1280]{3,2,1,0:T(8,128)(2,1)}) %all-gather.10.cloned.1.call-update) | async-done | bytes 2580496 | tf_op jit(solution)/shard_map/all_gather | solution.py:113
  206.5 2.0 reshape.869
  208.5 59.4 %all-gather.12.cloned.1.call-done = bf16[1280,1280]{1,0:T(8,128)(2,1)} async-done(((bf16[160,1280]{1,0:T(8,128)(2,1)}), bf16[1280,1280]{1,0:T(8,128)(2,1)}) %all-gather.12.cloned.1.call-update) | async-done | bytes 3276816 | tf_op jit(solution)/shard_map/all_gather | solution.py:119
  267.8 62.2 %all-gather.14.cloned.1.call-done = bf16[1280,1280]{0,1:T(8,128)(2,1)} async-done(((bf16[1280,160]{0,1:T(8,128)(2,1)}), bf16[1280,1280]{0,1:T(8,128)(2,1)}) %all-gather.14.cloned.1.call-update) | async-done | bytes 3276816 | tf_op jit(solution)/shard_map/all_gather | solution.py:126
  330.0 0.0 copy-done.7
  330.0 11.7 %fusion.20 = bf16[1,1008,1280]{2,1,0:T(8,128)(2,1)} fusion(bf16[1280,1280]{0,1:T(8,128)(2,1)} %all-gather.14.cloned.1.call-done, bf16[1008,1280]{1,0:T(8,128)(2,1)S(1)} %reshape.869, bf16[1280,1280]{1,0:T(8,128)(2,1)} %all-gather.12.cloned.1.call-done, f32[1280]{0:T(1024)S(1)} %copy-done.7), kind=kOutput, calls=%fused_computation.32 | convolution fusion | flops 6620221440 | bytes 11719680 | tf_op jit(solution)/shard_map/imf,fd->imd/dot_general | solution.py:123
  341.7 27.8 %fusion.1 = bf16[256,1280]{1,0:T(8,128)(2,1)S(1)} fusion(bf16[1,1008,1280]{2,1,0:T(8,128)(2,1)} %fusion.20), kind=kCustom, calls=%all-reduce-scatter.1 | all-reduce-scatter fusion | flops 1310721 | bytes 3236352
  369.6 4.4 %collective-permute-start.1 = (bf16[12,1280]{1,0:T(8,128)(2,1)S(1)}, bf16[12,1280]{1,0:T(8,128)(2,1)S(1)}, u32[]{:S(2)}, u32[]{:S(2)}) collective-permute-start(bf16[12,1280]{1,0:T(8,128)(2,1)S(1)} %slice.37), channel_id=1, source_target_pairs={{0,1},{1,2},{2,3},{4,5},{5,6},{6,7},{8,9},{9,10},{10,11},{12,13},{... | collective-permute-start | bytes 92168
  374.0 1.1 collective-permute-done.1
  375.1 1.0 concatenate.5
  376.1 1.3 add_convert_fusion.1
  (22 shorter events, 0.1 us)
Async XLA Ops:
  6.5 5.8 %copy-start = (f32[1,1024]{1,0:T(1,128)S(1)}, f32[1,1024]{1,0:T(1,128)}, u32[]{:S(2)}) copy-start(f32[1,1024]{1,0:T(1,128)} %param.13) | copy-start | bytes 12292
  6.5 5.9 %copy-start.8 = (s32[1,16]{1,0:T(1,128)S(1)}, s32[1,16]{1,0:T(1,128)}, u32[]{:S(2)}) copy-start(s32[1,16]{1,0:T(1,128)} %param.21) | copy-start | bytes 196
  6.5 6.5 %copy-start.3 = (s32[1,1008]{1,0:T(1,128)S(1)}, s32[1,1008]{1,0:T(1,128)}, u32[]{:S(2)}) copy-start(s32[1,1008]{1,0:T(1,128)} %param.23) | copy-start | bytes 12100
  6.5 8.1 %copy-start.5 = (s32[1,16]{1,0:T(1,128)S(1)}, s32[1,16]{1,0:T(1,128)}, u32[]{:S(2)}) copy-start(s32[1,16]{1,0:T(1,128)} %param.22) | copy-start | bytes 196
  6.5 8.3 %copy-start.2 = (bf16[320,160]{0,1:T(8,128)(2,1)S(1)}, bf16[320,160]{0,1:T(8,128)(2,1)}, u32[]{:S(2)}) copy-start(bf16[320,160]{0,1:T(8,128)(2,1)} %param.16) | copy-start | bytes 307204
  6.5 36.6 %all-gather.6.cloned.1.call-start = ((), (), s32[]{:S(2)}) async-start(), calls=%async_computation | async-start | bytes 3276800 | tf_op jit(solution)/shard_map/all_gather | solution.py:48
  11.6 86.2 %all-gather.8.cloned.1.call-start = ((), (), s32[]{:S(2)}) async-start(), calls=%async_computation.1 | async-start | bytes 3317760 | tf_op jit(solution)/shard_map/all_gather | solution.py:54
  12.3 194.2 %all-gather.10.cloned.1.call-start = ((), (), s32[]{:S(2)}) async-start(), calls=%async_computation.2 | async-start | bytes 3276800 | tf_op jit(solution)/shard_map/all_gather | solution.py:113
  113.2 5.8 %copy-start.9 = (f32[4,512,1024]{2,1,0:T(8,128)S(1)}, f32[4,512,1024]{2,1,0:T(8,128)}, u32[]{:S(2)}) copy-start(f32[4,512,1024]{2,1,0:T(8,128)} %get-tuple-element.11) | copy-start | bytes 25165828
  120.7 5.4 %copy-start.1 = (bf16[1,256,1280]{2,1,0:T(8,128)(2,1)S(1)}, bf16[1,256,1280]{2,1,0:T(8,128)(2,1)}, u32[]{:S(2)}) copy-start(bf16[1,256,1280]{2,1,0:T(8,128)(2,1)} %param.12) | copy-start | bytes 1966084
  145.1 31.8 %copy-start.6 = (u32[32]{0:T(128)S(1)}, u32[32]{0:T(128)}, u32[]{:S(2)}) copy-start(u32[32]{0:T(128)} %constant.99) | copy-start | bytes 388
  145.1 35.0 %copy-start.4 = (f32[1280]{0:T(1024)S(1)}, f32[1280]{0:T(1024)}, u32[]{:S(2)}) copy-start(f32[1280]{0:T(1024)} %param.17) | copy-start | bytes 15364
  172.5 5.7 %collective-permute-start = (bf16[12,1280]{1,0:T(8,128)(2,1)S(1)}, bf16[12,1280]{1,0:T(8,128)(2,1)S(1)}, u32[]{:S(2)}, u32[]{:S(2)}) collective-permute-start(bf16[12,1280]{1,0:T(8,128)(2,1)S(1)} %slice.36), channel_id=1, source_target_pairs={{0,1},{1,2},{2,3},{4,5},{5,6},{6,7},{8,9},{9,10},{10,11},{12,13},{... | collective-permute-start | bytes 92168
  181.4 148.7 %copy-start.7 = (f32[1280]{0:T(1024)S(1)}, f32[1280]{0:T(1024)}, u32[]{:S(2)}) copy-start(f32[1280]{0:T(1024)} %param.19) | copy-start | bytes 15364
  181.4 86.4 %all-gather.12.cloned.1.call-start = ((), (), s32[]{:S(2)}) async-start(), calls=%async_computation.3 | async-start | bytes 3686400 | tf_op jit(solution)/shard_map/all_gather | solution.py:119
  182.0 148.0 %all-gather.14.cloned.1.call-start = ((), (), s32[]{:S(2)}) async-start(), calls=%async_computation.4 | async-start | bytes 3686400 | tf_op jit(solution)/shard_map/all_gather | solution.py:126
  369.6 5.5 %collective-permute-start.1 = (bf16[12,1280]{1,0:T(8,128)(2,1)S(1)}, bf16[12,1280]{1,0:T(8,128)(2,1)S(1)}, u32[]{:S(2)}, u32[]{:S(2)}) collective-permute-start(bf16[12,1280]{1,0:T(8,128)(2,1)S(1)} %slice.37), channel_id=1, source_target_pairs={{0,1},{1,2},{2,3},{4,5},{5,6},{6,7},{8,9},{9,10},{10,11},{12,13},{... | collective-permute-start | bytes 92168
Sparse Core Ops, SparseCore 0:
  11.7 27.9 all-gather.5
  41.9 55.8 all-gather.7
  181.5 24.8 all-gather.9
  208.5 59.2 all-gather.11
  269.9 60.1 all-gather.13
